TPU v7x, 512 devices: a whole 4x4x16 slice. The times are simulated.
512 devices in a mesh: nodes: 128 (over z, x, core), mp: 4 (over y).
Axes of the slice: x: 4, y: 4, z: 16, core: 2. Of those that a mesh axis runs over, the one named last changes fastest.
Arguments:
- grid_in: bfloat16 [131072, 1024], P('nodes', 'mp'), may hold values from -2200 to 2200
- mesh_in: bfloat16 [32768, 1024], P('nodes', 'mp'), may hold values from -2200 to 2200
- w_query: bfloat16 [4, 1024, 512], P(None, None, 'mp'), as said below
- w_key: bfloat16 [4, 1024, 512], P(None, None, 'mp'), may hold values from -8 to 8
- w_value: bfloat16 [4, 1024, 512], P(None, None, 'mp'), may hold values from -0.1875 to 0.1875
- w_out: bfloat16 [4, 512, 1024], P(None, 'mp'), may hold values from -1 to 1
- norm_gains: float32 [6, 1024], replicated, may hold values from 0.25 to 1.75
- enc_list: int32 [256, 4], P('nodes'), may hold values from 0 to 1023, as said below
- proc_list: int32 [256, 3], P('nodes'), may hold values from 0 to 255, as said below
- dec_list: int32 [1024, 2], P('nodes'), may hold values from 0 to 255, as said below
- grid_count: int32 [1024], replicated, may hold values from 1 to 128
Outputs:
- grid_out: bfloat16 [131072, 1024], P('nodes', 'mp')
- mesh_out: bfloat16 [32768, 1024], P('nodes', 'mp')
Inputs may be any that keep to these rules, and one draw needn't show every extreme that they name: `enc_list`: mesh block b lies with node index b // 2; its 4 entries are distinct grid blocks held by node indices at most 2 from it (grid block c lies with node index c // 8). `proc_list`: entry 0 of row b is b; the others are distinct mesh blocks other than b held by node indices at most 2 from b's. `dec_list`: grid block c's 2 entries are distinct mesh blocks held by node indices at most 2 from c's. `w_query`: entries within 6 / sqrt(1024) of zero.
All inputs are finite; a program needn't handle non-finite values.
Results may differ from a plain program's by a relative error of at most 0.019.
Values may be sent and summed in bfloat16 or wider, within the bound.
No kernel may reach another device: no remote copies, remote signals or barrier semaphores. Data moves between devices by JAX's collectives and lax.ppermute only.
A program may use at most 64 MiB of HBM per device.

v0:
```python
import jax
import jax.numpy as jnp
from jax import lax
from jax.sharding import PartitionSpec as P

HEAD_DIM = 64
BLOCK = 128
REACH = 2
epsilon = 1e-05


def in_blocks(value, dim, count):
    lengths = value.shape
    pieces = value.reshape(*lengths[:dim], count, lengths[dim] // count, *lengths[dim + 1 :])
    return jnp.moveaxis(pieces, dim, 0)


def summed_on_arrival(value, axis, dim):
    pieces = in_blocks(value, dim, lax.axis_size(axis))
    arrived = lax.all_to_all(pieces, axis, split_axis=0, concat_axis=0, tiled=True)
    return arrived.astype(jnp.float32).sum(axis=0)


def from_behind(value, axis, steps):
    count = lax.axis_size(axis)
    first, last = (max(0, -steps), min(count, count - steps))
    return lax.ppermute(value, axis, [(source, source + steps) for source in range(first, last)])


def normalize(states, gains):
    values = states.astype(jnp.float32)
    average = jnp.mean(values, axis=-1, keepdims=True)
    centred = values - average
    spread = jnp.mean(centred * centred, axis=-1, keepdims=True)
    return (centred * lax.rsqrt(spread + epsilon) * gains).astype(jnp.bfloat16)


def project(inputs, weight):
    return jnp.dot(inputs, weight, preferred_element_type=jnp.float32).astype(jnp.bfloat16)


def attend(queries, key_rows, values, key_ok):
    batch_count, row_count, head_width = queries.shape
    key_count = key_rows.shape[1]
    head_count = head_width // HEAD_DIM
    query_heads = queries.reshape(batch_count, row_count, head_count, HEAD_DIM)
    key_heads = key_rows.reshape(batch_count, key_count, head_count, HEAD_DIM)
    value_heads = values.reshape(batch_count, key_count, head_count, HEAD_DIM)
    scores = jnp.einsum(
        "brhd,bkhd->bhrk", query_heads, key_heads, preferred_element_type=jnp.float32
    ) * HEAD_DIM ** (-0.5)
    if key_ok is not None:
        scores = jnp.where(key_ok[:, None, None, :], scores, -1e30)
    highest = jnp.max(scores, axis=-1, keepdims=True)
    weights = jnp.exp(scores - highest)
    chances = (weights / jnp.sum(weights, axis=-1, keepdims=True)).astype(jnp.bfloat16)
    blended = jnp.einsum(
        "bhrk,bkhd->brhd", chances, value_heads, preferred_element_type=jnp.float32
    )
    return blended.astype(jnp.bfloat16).reshape(batch_count * row_count, head_width)


def window(inputs, fetch):
    pieces = []
    for offset in range(-REACH, REACH + 1):
        pieces.append(inputs if offset == 0 else fetch(inputs, offset))
    return jnp.concatenate(pieces, axis=0)


def pick(beside_all, listed, window_start):
    blocks = beside_all.reshape(-1, BLOCK, beside_all.shape[1])
    local_ids = listed - window_start
    chosen = jnp.take(blocks, local_ids, axis=0)
    return chosen.reshape(listed.shape[0], listed.shape[1] * BLOCK, beside_all.shape[1])


def keys_values(normed, key_weight, value_weight):
    return jnp.concatenate([project(normed, key_weight), project(normed, value_weight)], axis=1)


def listed_valid(listed, grid_count):
    every_block = jnp.arange(grid_count.shape[0])
    counts = jnp.sum(
        jnp.where(listed[:, :, None] == every_block[None, None, :], grid_count[None, None, :], 0),
        axis=-1,
    )
    return jnp.arange(BLOCK)[None, None, :] < counts[:, :, None]


def per_device(
    grid_in,
    mesh_in,
    w_query,
    w_key,
    w_value,
    w_out,
    norm_gains,
    enc_list,
    proc_list,
    dec_list,
    grid_count,
):
    node_index = lax.axis_index("nodes")
    head_width = w_query.shape[2]
    grid_blocks = grid_in.shape[0] // BLOCK
    mesh_blocks = mesh_in.shape[0] // BLOCK
    grid_full, mesh_full = (
        lax.all_gather(grid_in, "mp", axis=1, tiled=True),
        lax.all_gather(mesh_in, "mp", axis=1, tiled=True),
    )
    own_counts = lax.dynamic_slice_in_dim(grid_count, node_index * grid_blocks, grid_blocks)
    row_ok = (jnp.arange(BLOCK)[None, :] < own_counts[:, None]).reshape(-1, 1)

    def mesh_update(blended, layer_index, state_part):
        whole_new = None
        terms = jnp.dot(blended, w_out[layer_index], preferred_element_type=jnp.float32)
        shares = summed_on_arrival(terms.astype(jnp.bfloat16), "mp", 1)
        part_new = (state_part.astype(jnp.float32) + shares).astype(jnp.bfloat16)
        whole_new = lax.all_gather(part_new, "mp", axis=1, tiled=True)
        return (part_new, whole_new)

    mesh_queries = project(normalize(mesh_full, norm_gains[0]), w_query[0]).reshape(
        mesh_blocks, BLOCK, head_width
    )
    grid_normed = normalize(grid_full, norm_gains[1])
    grid_kv = keys_values(grid_normed, w_key[0], w_value[0])
    listed_ok = listed_valid(enc_list, grid_count).reshape(enc_list.shape[0], -1)
    beside_all = window(grid_kv, lambda inputs, offset: from_behind(inputs, "nodes", -offset))
    chosen = pick(beside_all, enc_list, (node_index - REACH) * grid_blocks)
    blended = attend(mesh_queries, chosen[:, :, :head_width], chosen[:, :, head_width:], listed_ok)
    state_part, state_whole = mesh_update(blended, 0, mesh_in)
    for layer_index in (1, 2):
        normed = normalize(state_whole, norm_gains[layer_index + 1])
        queries = project(normed, w_query[layer_index]).reshape(mesh_blocks, BLOCK, head_width)
        mesh_kv = keys_values(normed, w_key[layer_index], w_value[layer_index])
        beside_all = window(mesh_kv, lambda inputs, offset: from_behind(inputs, "nodes", -offset))
        chosen = pick(beside_all, proc_list, (node_index - REACH) * mesh_blocks)
        blended = attend(queries, chosen[:, :, :head_width], chosen[:, :, head_width:], None)
        state_part, state_whole = mesh_update(blended, layer_index, state_part)
    grid_queries = project(normalize(grid_full, norm_gains[4]), w_query[3]).reshape(
        grid_blocks, BLOCK, head_width
    )
    mesh_normed = normalize(state_whole, norm_gains[5])
    mesh_kv = keys_values(mesh_normed, w_key[3], w_value[3])
    beside_all = window(mesh_kv, lambda inputs, offset: from_behind(inputs, "nodes", -offset))
    chosen = pick(beside_all, dec_list, (node_index - REACH) * mesh_blocks)
    blended = attend(grid_queries, chosen[:, :, :head_width], chosen[:, :, head_width:], None)
    terms = jnp.dot(blended, w_out[3], preferred_element_type=jnp.float32)
    update = lax.psum_scatter(
        terms.astype(jnp.bfloat16), "mp", scatter_dimension=1, tiled=True
    ).astype(jnp.float32)
    grid_out = grid_in.astype(jnp.float32) + update
    grid_out = jnp.where(row_ok, grid_out, 0.0).astype(jnp.bfloat16)
    return (grid_out, state_part)


def solution(mesh):
    placed = (
        P("nodes", "mp"),
        P("nodes", "mp"),
        P(None, None, "mp"),
        P(None, None, "mp"),
        P(None, None, "mp"),
        P(None, "mp", None),
        P(),
        P("nodes", None),
        P("nodes", None),
        P("nodes", None),
        P(),
    )
    return jax.shard_map(
        per_device,
        mesh=mesh,
        in_specs=placed,
        out_specs=(P("nodes", "mp"), P("nodes", "mp")),
        check_vma=False,
    )
```

profile of v0, /device:TPU:1, one launch (start us, length us, event | category | flops | bytes accessed | tf_op | source)
XLA Modules:
  0.0 329.7 jit_solution(16877713221942611837)
XLA Ops:
  8.8 11.4 %all_gather.16 = bf16[256,1024]{1,0:T(8,128)(2,1)S(1)} all-gather(bf16[256,256]{1,0:T(8,128)(2,1)} %param.14), channel_id=1, replica_groups=mesh['nodes'=128,'mp'=4] {'mp'}, dimensions={1}, use_global_device_ids=true | all-gather | bytes 655360 | tf_op jit(solution)/shard_map/all_gather | solution.py:109
  20.8 1.6 fusion.139
  22.4 1.3 convolution_convert_fusion.18
  23.7 31.9 %all-gather.2.cloned.1.call-done = bf16[1024,1024]{1,0:T(8,128)(2,1)} async-done(((bf16[1024,256]{1,0:T(8,128)(2,1)}), bf16[1024,1024]{1,0:T(8,128)(2,1)}) %all-gather.2.cloned.1.call-update) | async-done | bytes 2097168 | tf_op jit(solution)/shard_map/all_gather | solution.py:108
  55.7 2.1 convert_reduce_fusion
  59.3 1.8 convolution_convert_fusion.5
  61.1 1.8 convolution_convert_fusion.6
  62.9 5.0 %collective-permute-start.1 = (bf16[1024,256]{0,1:T(8,128)(2,1)S(1)}, bf16[1024,256]{0,1:T(8,128)(2,1)}, u32[]{:S(2)}, u32[]{:S(2)}) collective-permute-start(bf16[1024,256]{0,1:T(8,128)(2,1)S(1)} %pad_maximum_fusion), channel_id=1, source_target_pairs={{0,4},{4,8},{8,12},{12,16},{16,20},{20,24},{24,28},{28,32},{32,36}... | collective-permute-start | bytes 1572872 | tf_op jit(solution)/shard_map/ppermute | solution.py:27
  68.0 3.9 %collective-permute-start = (bf16[1024,256]{0,1:T(8,128)(2,1)S(1)}, bf16[1024,256]{0,1:T(8,128)(2,1)}, u32[]{:S(2)}, u32[]{:S(2)}) collective-permute-start(bf16[1024,256]{0,1:T(8,128)(2,1)S(1)} %pad_maximum_fusion), channel_id=1, source_target_pairs={{0,8},{4,12},{8,16},{12,20},{16,24},{20,28},{24,32},{28,36},{32,40... | collective-permute-start | bytes 1572872 | tf_op jit(solution)/shard_map/ppermute | solution.py:27
  71.9 1.9 collective-permute-start.2
  73.9 1.3 collective-permute-start.3
  75.4 9.9 %collective-permute-done = bf16[1024,256]{0,1:T(8,128)(2,1)} collective-permute-done((bf16[1024,256]{0,1:T(8,128)(2,1)S(1)}, bf16[1024,256]{0,1:T(8,128)(2,1)}, u32[]{:S(2)}, u32[]{:S(2)}) %collective-permute-start) | collective-permute-done | bytes 524320 | tf_op jit(solution)/shard_map/ppermute | solution.py:27
  85.3 1.9 constant_dynamic-update-slice_fusion.4
  87.2 1.9 constant_dynamic-update-slice_fusion.3
  90.0 1.9 constant_dynamic-update-slice_fusion.1
  91.9 1.9 constant_dynamic-update-slice_fusion
  93.8 4.4 %copy.97 = bf16[5120,256]{1,0:T(8,128)(2,1)} copy(bf16[5120,256]{0,1:T(8,128)(2,1)} %constant_dynamic-update-slice_fusion) | data formatting | bytes 5242880 | tf_op jit(solution)/shard_map/reshape | solution.py:71
  98.2 2.3 gather_fusion
  101.5 1.1 fusion.140
  103.6 2.0 fusion.36
  105.7 1.3 convolution_convert_fusion.3
  107.8 3.7 %all-to-all-start = ((bf16[4,256,256]{2,1,0:T(8,128)(2,1)}), bf16[4,256,256]{2,1,0:T(8,128)(2,1)S(1)}, u32[]{:S(2)}, u32[]{:S(2)}) async-start(bf16[4,256,256]{2,1,0:T(8,128)(2,1)} %bitcast.165), calls=%async_computation | async-start | bytes 1048576 | tf_op jit(solution)/shard_map/all_to_all | solution.py:20
  112.9 5.5 %all-to-all-done = bf16[4,256,256]{2,1,0:T(8,128)(2,1)S(1)} async-done(((bf16[4,256,256]{2,1,0:T(8,128)(2,1)}), bf16[4,256,256]{2,1,0:T(8,128)(2,1)S(1)}, u32[]{:S(2)}, u32[]{:S(2)}) %all-to-all-start) | async-done | bytes 524320 | tf_op jit(solution)/shard_map/all_to_all | solution.py:20
  118.5 10.1 %all_gather.17 = bf16[256,1024]{1,0:T(8,128)(2,1)S(1)} all-gather(bf16[256,256]{1,0:T(8,128)(2,1)S(1)} %add_convert_fusion.2), channel_id=1, replica_groups=mesh['nodes'=128,'mp'=4] {'mp'}, dimensions={1}, use_global_device_ids=true | all-gather | bytes 655360 | tf_op jit(solution)/shard_map/all_gather | solution.py:119
  129.4 1.3 convolution_convert_fusion.15
  130.7 1.3 convolution_convert_fusion.16
  131.9 10.9 %collective-permute-start.5 = (bf16[256,256]{0,1:T(8,128)(2,1)S(1)}, bf16[256,256]{0,1:T(8,128)(2,1)S(1)}, u32[]{:S(2)}, u32[]{:S(2)}) collective-permute-start(bf16[256,256]{0,1:T(8,128)(2,1)S(1)} %pad_maximum_fusion.1), channel_id=1, source_target_pairs={{0,4},{4,8},{8,12},{12,16},{16,20},{20,24},{24,28},{28,32},{32,36}... | collective-permute-start | bytes 393224 | tf_op jit(solution)/shard_map/ppermute | solution.py:27
  142.9 3.2 collective-permute-start.4
  146.1 1.2 convolution_convert_fusion.14
  147.3 1.3 collective-permute-start.7
  148.6 1.9 collective-permute-start.6
  153.3 2.1 collective-permute-done.6
  156.8 1.4 copy.77
  159.1 1.4 fusion.143
  160.9 1.0 fusion.37
  162.0 1.3 convolution_convert_fusion.2
  163.3 10.8 %all_to_all.15 = bf16[4,256,256]{2,1,0:T(8,128)(2,1)S(1)} all-to-all(bf16[4,256,256]{2,1,0:T(8,128)(2,1)S(1)} %bitcast.173), channel_id=1, replica_groups=mesh['nodes'=128,'mp'=4] {'mp'}, dimensions={0} | all-to-all | bytes 1048576 | tf_op jit(solution)/shard_map/all_to_all | solution.py:20
  174.2 11.8 %all_gather.18 = bf16[256,1024]{1,0:T(8,128)(2,1)S(1)} all-gather(bf16[256,256]{1,0:T(8,128)(2,1)S(1)} %add_convert_fusion.1), channel_id=1, replica_groups=mesh['nodes'=128,'mp'=4] {'mp'}, dimensions={1}, use_global_device_ids=true | all-gather | bytes 655360 | tf_op jit(solution)/shard_map/all_gather | solution.py:119
  186.8 1.3 convolution_convert_fusion.11
  188.1 1.3 convolution_convert_fusion.12
  189.4 5.1 %collective-permute-start.9 = (bf16[256,256]{0,1:T(8,128)(2,1)S(1)}, bf16[256,256]{0,1:T(8,128)(2,1)S(1)}, u32[]{:S(2)}, u32[]{:S(2)}) collective-permute-start(bf16[256,256]{0,1:T(8,128)(2,1)S(1)} %pad_maximum_fusion.2), channel_id=1, source_target_pairs={{0,4},{4,8},{8,12},{12,16},{16,20},{20,24},{24,28},{28,32},{32,36}... | collective-permute-start | bytes 393224 | tf_op jit(solution)/shard_map/ppermute | solution.py:27
  194.5 4.2 %collective-permute-start.8 = (bf16[256,256]{0,1:T(8,128)(2,1)S(1)}, bf16[256,256]{0,1:T(8,128)(2,1)S(1)}, u32[]{:S(2)}, u32[]{:S(2)}) collective-permute-start(bf16[256,256]{0,1:T(8,128)(2,1)S(1)} %pad_maximum_fusion.2), channel_id=1, source_target_pairs={{0,8},{4,12},{8,16},{12,20},{16,24},{20,28},{24,32},{28,36},{32,40... | collective-permute-start | bytes 393224 | tf_op jit(solution)/shard_map/ppermute | solution.py:27
  198.6 1.2 convolution_convert_fusion.10
  199.9 1.3 collective-permute-start.11
  201.2 1.9 collective-permute-start.10
  205.3 2.3 collective-permute-done.10
  208.9 1.3 copy.84
  213.3 1.3 convolution_convert_fusion.1
  215.4 3.5 %all-to-all-start.2 = ((bf16[4,256,256]{2,1,0:T(8,128)(2,1)}), bf16[4,256,256]{2,1,0:T(8,128)(2,1)S(1)}, u32[]{:S(2)}, u32[]{:S(2)}) async-start(bf16[4,256,256]{2,1,0:T(8,128)(2,1)} %bitcast.161), calls=%async_computation.2 | async-start | bytes 1048576 | tf_op jit(solution)/shard_map/all_to_all | solution.py:20
  219.0 7.6 %all-to-all-done.2 = bf16[4,256,256]{2,1,0:T(8,128)(2,1)S(1)} async-done(((bf16[4,256,256]{2,1,0:T(8,128)(2,1)}), bf16[4,256,256]{2,1,0:T(8,128)(2,1)S(1)}, u32[]{:S(2)}, u32[]{:S(2)}) %all-to-all-start.2) | async-done | bytes 524320 | tf_op jit(solution)/shard_map/all_to_all | solution.py:20
  226.7 11.1 %all_gather.19 = bf16[256,1024]{1,0:T(8,128)(2,1)S(1)} all-gather(bf16[256,256]{1,0:T(8,128)(2,1)S(1)} %add_convert_fusion), channel_id=1, replica_groups=mesh['nodes'=128,'mp'=4] {'mp'}, dimensions={1}, use_global_device_ids=true | all-gather | bytes 655360 | tf_op jit(solution)/shard_map/all_gather | solution.py:119
  238.3 1.4 convolution_convert_fusion.7
  239.6 1.4 convolution_convert_fusion.8
  241.0 4.5 %collective-permute-start.13 = (bf16[256,256]{0,1:T(8,128)(2,1)S(1)}, bf16[256,256]{0,1:T(8,128)(2,1)S(1)}, u32[]{:S(2)}, u32[]{:S(2)}) collective-permute-start(bf16[256,256]{0,1:T(8,128)(2,1)S(1)} %pad_maximum_fusion.3), channel_id=1, source_target_pairs={{0,4},{4,8},{8,12},{12,16},{16,20},{20,24},{24,28},{28,32},{32,36}... | collective-permute-start | bytes 393224 | tf_op jit(solution)/shard_map/ppermute | solution.py:27
  245.5 5.6 %collective-permute-start.12 = (bf16[256,256]{0,1:T(8,128)(2,1)S(1)}, bf16[256,256]{0,1:T(8,128)(2,1)S(1)}, u32[]{:S(2)}, u32[]{:S(2)}) collective-permute-start(bf16[256,256]{0,1:T(8,128)(2,1)S(1)} %pad_maximum_fusion.3), channel_id=1, source_target_pairs={{0,8},{4,12},{8,16},{12,20},{16,24},{20,28},{24,32},{28,36},{32,40... | collective-permute-start | bytes 393224 | tf_op jit(solution)/shard_map/ppermute | solution.py:27
  251.2 1.8 fusion.32
  253.0 1.1 reshape.263
  254.0 1.3 collective-permute-start.15
  255.3 1.9 collective-permute-start.14
  257.3 5.2 %collective-permute-done.14 = bf16[256,256]{0,1:T(8,128)(2,1)S(1)} collective-permute-done((bf16[256,256]{0,1:T(8,128)(2,1)S(1)}, bf16[256,256]{0,1:T(8,128)(2,1)S(1)}, u32[]{:S(2)}, u32[]{:S(2)}) %collective-permute-start.14) | collective-permute-done | bytes 131104 | tf_op jit(solution)/shard_map/ppermute | solution.py:27
  266.4 3.7 %fusion.35 = bf16[8,128,2,64]{1,3,2,0:T(8,128)(2,1)S(1)} fusion(bf16[8,256,2,64]{1,3,2,0:T(8,128)(2,1)S(1)} %bitcast.190, f32[8,2,128]{2,1,0:T(2,128)S(1)} %fusion.149, bf16[8,256,2,64]{1,3,2,0:T(8,128)(2,1)S(1)} %bitcast.189, bf16[8,128,2,64]{3,2,1,0:T(2,128)(2,1)S(1)} %copy-done.3), kind=kOutput, calls=%fused_computation.59 | convolution fusion | flops 136448256 | bytes 1581056 | tf_op jit(solution)/shard_map/bhrk,bkhd->brhd/dot_general | solution.py:57
  270.3 3.0 convolution_convert_fusion
  274.2 46.6 %reduce-scatter.2.cloned.1.call-done = bf16[1024,256]{1,0:T(8,128)(2,1)} async-done(((bf16[1024,1024]{1,0:T(8,128)(2,1)}), bf16[1024,256]{1,0:T(8,128)(2,1)}) %reduce-scatter.2.cloned.1.call-update) | async-done | bytes 524304 | tf_op jit(solution)/shard_map/reduce_scatter | solution.py:149
  320.9 2.0 select_convert_fusion
  (150 shorter events, 29.4 us)
Async XLA Ops:
  7.2 48.5 %all-gather.2.cloned.1.call-start = ((), (), s32[]{:S(2)}) async-start(), calls=%async_computation.4 | async-start | bytes 2621440 | tf_op jit(solution)/shard_map/all_gather | solution.py:108
  20.8 80.7 %copy-start.8 = (pred[2,512]{1,0:T(4,128)(4,1)}, pred[2,512]{1,0:T(4,128)(4,1)S(1)}, u32[]{:S(2)}) copy-start(pred[2,512]{1,0:T(4,128)(4,1)S(1)} %bitcast_compare_fusion) | copy-start | bytes 3076
  55.7 2.2 copy-start
  59.3 12.6 %copy-start.13 = (s32[2,4]{1,0:T(2,128)S(1)}, s32[2,4]{1,0:T(2,128)}, u32[]{:S(2)}) copy-start(s32[2,4]{1,0:T(2,128)} %param.20) | copy-start | bytes 100
  62.9 24.3 %collective-permute-start.1 = (bf16[1024,256]{0,1:T(8,128)(2,1)S(1)}, bf16[1024,256]{0,1:T(8,128)(2,1)}, u32[]{:S(2)}, u32[]{:S(2)}) collective-permute-start(bf16[1024,256]{0,1:T(8,128)(2,1)S(1)} %pad_maximum_fusion), channel_id=1, source_target_pairs={{0,4},{4,8},{8,12},{12,16},{16,20},{20,24},{24,28},{28,32},{32,36}... | collective-permute-start | bytes 1572872 | tf_op jit(solution)/shard_map/ppermute | solution.py:27
  68.0 17.3 %collective-permute-start = (bf16[1024,256]{0,1:T(8,128)(2,1)S(1)}, bf16[1024,256]{0,1:T(8,128)(2,1)}, u32[]{:S(2)}, u32[]{:S(2)}) collective-permute-start(bf16[1024,256]{0,1:T(8,128)(2,1)S(1)} %pad_maximum_fusion), channel_id=1, source_target_pairs={{0,8},{4,12},{8,16},{12,20},{16,24},{20,28},{24,32},{28,36},{32,40... | collective-permute-start | bytes 1572872 | tf_op jit(solution)/shard_map/ppermute | solution.py:27
  71.9 18.1 %collective-permute-start.2 = (bf16[1024,256]{0,1:T(8,128)(2,1)S(1)}, bf16[1024,256]{0,1:T(8,128)(2,1)}, u32[]{:S(2)}, u32[]{:S(2)}) collective-permute-start(bf16[1024,256]{0,1:T(8,128)(2,1)S(1)} %pad_maximum_fusion), channel_id=1, source_target_pairs={{4,0},{8,4},{12,8},{16,12},{20,16},{24,20},{28,24},{32,28},{36,32}... | collective-permute-start | bytes 1572872 | tf_op jit(solution)/shard_map/ppermute | solution.py:27
  73.9 17.9 %collective-permute-start.3 = (bf16[1024,256]{0,1:T(8,128)(2,1)S(1)}, bf16[1024,256]{0,1:T(8,128)(2,1)}, u32[]{:S(2)}, u32[]{:S(2)}) collective-permute-start(bf16[1024,256]{0,1:T(8,128)(2,1)S(1)} %pad_maximum_fusion), channel_id=1, source_target_pairs={{8,0},{12,4},{16,8},{20,12},{24,16},{28,20},{32,24},{36,28},{40,32... | collective-permute-start | bytes 1572872 | tf_op jit(solution)/shard_map/ppermute | solution.py:27
  105.6 5.9 %copy-start.15 = (s32[2,3]{1,0:T(2,128)S(1)}, s32[2,3]{1,0:T(2,128)}, u32[]{:S(2)}) copy-start(s32[2,3]{1,0:T(2,128)} %param.21) | copy-start | bytes 76
  105.6 6.0 %copy-start.16 = (s32[8,2]{0,1:T(2,128)S(1)}, s32[8,2]{0,1:T(2,128)}, u32[]{:S(2)}) copy-start(s32[8,2]{0,1:T(2,128)} %param.22) | copy-start | bytes 196
  105.6 12.9 %copy-start.4 = (bf16[256,256]{1,0:T(8,128)(2,1)S(1)}, bf16[256,256]{1,0:T(8,128)(2,1)}, u32[]{:S(2)}) copy-start(bf16[256,256]{1,0:T(8,128)(2,1)} %param.14) | copy-start | bytes 393220
  107.8 10.6 %all-to-all-start = ((bf16[4,256,256]{2,1,0:T(8,128)(2,1)}), bf16[4,256,256]{2,1,0:T(8,128)(2,1)S(1)}, u32[]{:S(2)}, u32[]{:S(2)}) async-start(bf16[4,256,256]{2,1,0:T(8,128)(2,1)} %bitcast.165), calls=%async_computation | async-start | bytes 1048576 | tf_op jit(solution)/shard_map/all_to_all | solution.py:20
  111.5 47.2 %copy-start.9 = (pred[2,3]{1,0:T(4,128)(4,1)}, pred[2,3]{1,0:T(4,128)(4,1)S(1)}, u32[]{:S(2)}) copy-start(pred[2,3]{1,0:T(4,128)(4,1)S(1)} %get-tuple-element.5) | copy-start | bytes 22
  112.9 45.3 %copy-start.7 = (s32[1024]{0:T(1024)}, s32[1024]{0:T(1024)S(1)}, u32[]{:S(2)}) copy-start(s32[1024]{0:T(1024)S(1)} %get-tuple-element.24) | copy-start | bytes 12292
  131.9 20.0 %collective-permute-start.5 = (bf16[256,256]{0,1:T(8,128)(2,1)S(1)}, bf16[256,256]{0,1:T(8,128)(2,1)S(1)}, u32[]{:S(2)}, u32[]{:S(2)}) collective-permute-start(bf16[256,256]{0,1:T(8,128)(2,1)S(1)} %pad_maximum_fusion.1), channel_id=1, source_target_pairs={{0,4},{4,8},{8,12},{12,16},{16,20},{20,24},{24,28},{28,32},{32,36}... | collective-permute-start | bytes 393224 | tf_op jit(solution)/shard_map/ppermute | solution.py:27
  142.9 8.4 %collective-permute-start.4 = (bf16[256,256]{0,1:T(8,128)(2,1)S(1)}, bf16[256,256]{0,1:T(8,128)(2,1)S(1)}, u32[]{:S(2)}, u32[]{:S(2)}) collective-permute-start(bf16[256,256]{0,1:T(8,128)(2,1)S(1)} %pad_maximum_fusion.1), channel_id=1, source_target_pairs={{0,8},{4,12},{8,16},{12,20},{16,24},{20,28},{24,32},{28,36},{32,40... | collective-permute-start | bytes 393224 | tf_op jit(solution)/shard_map/ppermute | solution.py:27
  147.3 8.8 %collective-permute-start.7 = (bf16[256,256]{0,1:T(8,128)(2,1)S(1)}, bf16[256,256]{0,1:T(8,128)(2,1)S(1)}, u32[]{:S(2)}, u32[]{:S(2)}) collective-permute-start(bf16[256,256]{0,1:T(8,128)(2,1)S(1)} %pad_maximum_fusion.1), channel_id=1, source_target_pairs={{8,0},{12,4},{16,8},{20,12},{24,16},{28,20},{32,24},{36,28},{40,32... | collective-permute-start | bytes 393224 | tf_op jit(solution)/shard_map/ppermute | solution.py:27
  148.6 6.8 %collective-permute-start.6 = (bf16[256,256]{0,1:T(8,128)(2,1)S(1)}, bf16[256,256]{0,1:T(8,128)(2,1)S(1)}, u32[]{:S(2)}, u32[]{:S(2)}) collective-permute-start(bf16[256,256]{0,1:T(8,128)(2,1)S(1)} %pad_maximum_fusion.1), channel_id=1, source_target_pairs={{4,0},{8,4},{12,8},{16,12},{20,16},{24,20},{28,24},{32,28},{36,32}... | collective-permute-start | bytes 393224 | tf_op jit(solution)/shard_map/ppermute | solution.py:27
  156.8 3.7 %copy-start.2 = (bf16[2,128,2,64]{3,2,1,0:T(2,128)(2,1)S(1)}, bf16[2,128,2,64]{3,2,1,0:T(2,128)(2,1)}, u32[]{:S(2)}) copy-start(bf16[2,128,2,64]{3,2,1,0:T(2,128)(2,1)} %reshape.261) | copy-start | bytes 196612
  188.1 22.8 %copy-start.10 = (pred[2,3]{1,0:T(4,128)(4,1)S(1)}, pred[2,3]{1,0:T(4,128)(4,1)}, u32[]{:S(2)}) copy-start(pred[2,3]{1,0:T(4,128)(4,1)} %copy-done.9) | copy-start | bytes 22
  189.4 14.5 %collective-permute-start.9 = (bf16[256,256]{0,1:T(8,128)(2,1)S(1)}, bf16[256,256]{0,1:T(8,128)(2,1)S(1)}, u32[]{:S(2)}, u32[]{:S(2)}) collective-permute-start(bf16[256,256]{0,1:T(8,128)(2,1)S(1)} %pad_maximum_fusion.2), channel_id=1, source_target_pairs={{0,4},{4,8},{8,12},{12,16},{16,20},{20,24},{24,28},{28,32},{32,36}... | collective-permute-start | bytes 393224 | tf_op jit(solution)/shard_map/ppermute | solution.py:27
  194.5 8.8 %collective-permute-start.8 = (bf16[256,256]{0,1:T(8,128)(2,1)S(1)}, bf16[256,256]{0,1:T(8,128)(2,1)S(1)}, u32[]{:S(2)}, u32[]{:S(2)}) collective-permute-start(bf16[256,256]{0,1:T(8,128)(2,1)S(1)} %pad_maximum_fusion.2), channel_id=1, source_target_pairs={{0,8},{4,12},{8,16},{12,20},{16,24},{20,28},{24,32},{28,36},{32,40... | collective-permute-start | bytes 393224 | tf_op jit(solution)/shard_map/ppermute | solution.py:27
  199.9 8.3 %collective-permute-start.11 = (bf16[256,256]{0,1:T(8,128)(2,1)S(1)}, bf16[256,256]{0,1:T(8,128)(2,1)S(1)}, u32[]{:S(2)}, u32[]{:S(2)}) collective-permute-start(bf16[256,256]{0,1:T(8,128)(2,1)S(1)} %pad_maximum_fusion.2), channel_id=1, source_target_pairs={{8,0},{12,4},{16,8},{20,12},{24,16},{28,20},{32,24},{36,28},{40,32... | collective-permute-start | bytes 393224 | tf_op jit(solution)/shard_map/ppermute | solution.py:27
  201.2 6.4 %collective-permute-start.10 = (bf16[256,256]{0,1:T(8,128)(2,1)S(1)}, bf16[256,256]{0,1:T(8,128)(2,1)S(1)}, u32[]{:S(2)}, u32[]{:S(2)}) collective-permute-start(bf16[256,256]{0,1:T(8,128)(2,1)S(1)} %pad_maximum_fusion.2), channel_id=1, source_target_pairs={{4,0},{8,4},{12,8},{16,12},{20,16},{24,20},{28,24},{32,28},{36,32}... | collective-permute-start | bytes 393224 | tf_op jit(solution)/shard_map/ppermute | solution.py:27
  212.2 6.8 %copy-start.14 = (pred[8,2]{0,1:T(4,128)(4,1)S(1)}, pred[8,2]{0,1:T(4,128)(4,1)}, u32[]{:S(2)}) copy-start(pred[8,2]{0,1:T(4,128)(4,1)} %get-tuple-element.3) | copy-start | bytes 52
  214.6 23.7 %copy-start.12 = (f32[1,1024]{1,0:T(1,128)S(1)}, f32[1,1024]{1,0:T(1,128)}, u32[]{:S(2)}) copy-start(f32[1,1024]{1,0:T(1,128)} %get-tuple-element.22) | copy-start | bytes 12292
  215.4 11.2 %all-to-all-start.2 = ((bf16[4,256,256]{2,1,0:T(8,128)(2,1)}), bf16[4,256,256]{2,1,0:T(8,128)(2,1)S(1)}, u32[]{:S(2)}, u32[]{:S(2)}) async-start(bf16[4,256,256]{2,1,0:T(8,128)(2,1)} %bitcast.161), calls=%async_computation.2 | async-start | bytes 1048576 | tf_op jit(solution)/shard_map/all_to_all | solution.py:20
  218.9 102.0 %reduce-scatter.2.cloned.1.call-start = ((), (), s32[]{:S(2)}) async-start(), calls=%async_computation.5 | async-start | bytes 2621440 | tf_op jit(solution)/shard_map/reduce_scatter | solution.py:149
  226.7 26.3 %copy-start.5 = (bf16[256,256]{1,0:T(8,128)(2,1)}, bf16[256,256]{1,0:T(8,128)(2,1)S(1)}, u32[]{:S(2)}) copy-start(bf16[256,256]{1,0:T(8,128)(2,1)S(1)} %add_convert_fusion) | copy-start | bytes 393220
  226.7 24.4 %copy-start.11 = (f32[1,1024]{1,0:T(1,128)S(1)}, f32[1,1024]{1,0:T(1,128)}, u32[]{:S(2)}) copy-start(f32[1,1024]{1,0:T(1,128)} %get-tuple-element.17) | copy-start | bytes 12292
  241.0 16.2 %collective-permute-start.13 = (bf16[256,256]{0,1:T(8,128)(2,1)S(1)}, bf16[256,256]{0,1:T(8,128)(2,1)S(1)}, u32[]{:S(2)}, u32[]{:S(2)}) collective-permute-start(bf16[256,256]{0,1:T(8,128)(2,1)S(1)} %pad_maximum_fusion.3), channel_id=1, source_target_pairs={{0,4},{4,8},{8,12},{12,16},{16,20},{20,24},{24,28},{28,32},{32,36}... | collective-permute-start | bytes 393224 | tf_op jit(solution)/shard_map/ppermute | solution.py:27
  245.5 11.7 %collective-permute-start.12 = (bf16[256,256]{0,1:T(8,128)(2,1)S(1)}, bf16[256,256]{0,1:T(8,128)(2,1)S(1)}, u32[]{:S(2)}, u32[]{:S(2)}) collective-permute-start(bf16[256,256]{0,1:T(8,128)(2,1)S(1)} %pad_maximum_fusion.3), channel_id=1, source_target_pairs={{0,8},{4,12},{8,16},{12,20},{16,24},{20,28},{24,32},{28,36},{32,40... | collective-permute-start | bytes 393224 | tf_op jit(solution)/shard_map/ppermute | solution.py:27
  253.0 10.3 %copy-start.6 = (s32[1024]{0:T(1024)S(1)}, s32[1024]{0:T(1024)}, u32[]{:S(2)}) copy-start(s32[1024]{0:T(1024)} %get-tuple-element.23) | copy-start | bytes 12292
  254.0 9.0 %collective-permute-start.15 = (bf16[256,256]{0,1:T(8,128)(2,1)S(1)}, bf16[256,256]{0,1:T(8,128)(2,1)S(1)}, u32[]{:S(2)}, u32[]{:S(2)}) collective-permute-start(bf16[256,256]{0,1:T(8,128)(2,1)S(1)} %pad_maximum_fusion.3), channel_id=1, source_target_pairs={{8,0},{12,4},{16,8},{20,12},{24,16},{28,20},{32,24},{36,28},{40,32... | collective-permute-start | bytes 393224 | tf_op jit(solution)/shard_map/ppermute | solution.py:27
  255.3 7.2 %collective-permute-start.14 = (bf16[256,256]{0,1:T(8,128)(2,1)S(1)}, bf16[256,256]{0,1:T(8,128)(2,1)S(1)}, u32[]{:S(2)}, u32[]{:S(2)}) collective-permute-start(bf16[256,256]{0,1:T(8,128)(2,1)S(1)} %pad_maximum_fusion.3), channel_id=1, source_target_pairs={{4,0},{8,4},{12,8},{16,12},{20,16},{24,20},{28,24},{32,28},{36,32}... | collective-permute-start | bytes 393224 | tf_op jit(solution)/shard_map/ppermute | solution.py:27
  264.4 1.0 copy-start.3
  270.1 50.7 %copy-start.1 = (bf16[1024,256]{1,0:T(8,128)(2,1)S(1)}, bf16[1024,256]{1,0:T(8,128)(2,1)}, u32[]{:S(2)}) copy-start(bf16[1024,256]{1,0:T(8,128)(2,1)} %param.13) | copy-start | bytes 1572868
Sparse Core Ops, SparseCore 0:
  10.1 45.5 all-gather.1
  273.5 47.2 reduce-scatter.1
where the time goes:
time: 332 us; the launch traced here: 330 us
  waiting for transfers between devices  112 us (34%)
  starting transfers between devices  62.4 us (19%)
  blocking collectives  55.2 us (17%)
  matrix products  36.8 us (11%)
  local copies, waits for them, and re-layouts  35 us (11%)
  between operations  14.9 us (4%)
  other arithmetic  13.1 us (4%)
    ppermute x16, starting transfers between devices, from_behind(): lax.ppermute(value, axis, [(source, source + steps) for source in range(f...  55.2 us
    reduce_scatter x1, waiting for transfers between devices, per_device(): lax.psum_scatter(terms.astype(jnp.bfloat16), 'mp', scatter_dimension=1, t...  46.6 us
    all_gather x3, blocking collectives, mesh_update(): whole_new = lax.all_gather(part_new, 'mp', axis=1, tiled=True)  33 us
    all_gather x1, waiting for transfers between devices, per_device(): lax.all_gather(grid_in, 'mp', axis=1, tiled=True)  31.9 us
    ppermute x16, waiting for transfers between devices, from_behind(): lax.ppermute(value, axis, [(source, source + steps) for source in range(f...  20 us
    dot_general x12, matrix products, project(): jnp.dot(inputs, weight, preferred_element_type=jnp.float32)  16.9 us
    all_to_all x2, waiting for transfers between devices, summed_on_arrival(): lax.all_to_all(pieces, axis, split_axis=0, concat_axis=0, tiled=True)  13.1 us
    all_gather x1, blocking collectives, per_device(): lax.all_gather(mesh_in, 'mp', axis=1, tiled=True)  11.4 us
  transfers between devices with their start and end apart: 20, of which 9 were waited for; matrix products, arithmetic and copies ran while one was open for 8% of the time, Pallas kernels for 0%

commit v1 on v0

--- a/solution.py
+++ b/solution.py
@@ -105,7 +105,9 @@
     grid_blocks = grid_in.shape[0] // BLOCK
     mesh_blocks = mesh_in.shape[0] // BLOCK
     grid_full, mesh_full = (
-        lax.all_gather(grid_in, "mp", axis=1, tiled=True),
+        jnp.concatenate(
+            lax.all_to_all(jnp.stack([grid_in] * lax.axis_size("mp")), "mp", 0, 0), axis=1
+        ),
         lax.all_gather(mesh_in, "mp", axis=1, tiled=True),
     )
     own_counts = lax.dynamic_slice_in_dim(grid_count, node_index * grid_blocks, grid_blocks)

time: 332 us -> 310 us (0.934)
  waiting for transfers between devices: 112 us -> 89.5 us
  blocking collectives: 55.2 us -> 71.9 us
  local copies, waits for them, and re-layouts: 35 us -> 19.7 us
  starting transfers between devices: 62.4 us -> 72.3 us
  matrix products: 36.8 us -> 30.3 us
  other arithmetic: 13.1 us -> 9.53 us
    all_gather x1 -> x0, waiting for transfers between devices: 31.9 us -> none  [per_device(): lax.all_gather(grid_in, 'mp', axis=1, tiled=True)]
    all_gather x1, blocking collectives: 11.4 us -> 29.5 us  [per_device(): lax.all_gather(mesh_in, 'mp', axis=1, tiled=True)]
    ppermute x16, waiting for transfers between devices: 20 us -> 26.9 us  [from_behind(): lax.ppermute(value, axis, [(source, source + steps) for source in range(f...]
    unnamed x49 -> x36, local copies, waits for them, and re-layouts: 10.9 us -> 4.8 us
    all_to_all x0 -> x1, starting transfers between devices: none -> 5.14 us  [per_device(): lax.all_to_all(jnp.stack([grid_in] * lax.axis_size('mp')), 'mp', 0, 0)]
    ppermute x16, starting transfers between devices: 55.2 us -> 60.1 us  [from_behind(): lax.ppermute(value, axis, [(source, source + steps) for source in range(f...]
    concatenate x7, local copies, waits for them, and re-layouts: 6.18 us -> 1.82 us  [window(): return jnp.concatenate(pieces, axis=0)]
  transfers between devices with their start and end apart: 20 -> 20, of which waited for: 9 -> 10; matrix products, arithmetic and copies ran while one was open for 8% -> 4% of each run, Pallas kernels for 0% -> 0%
where the time goes in v1:
time: 310 us; the launch traced here: 308 us
  waiting for transfers between devices  89.5 us (29%)
  starting transfers between devices  72.3 us (23%)
  blocking collectives  71.9 us (23%)
  matrix products  30.3 us (10%)
  local copies, waits for them, and re-layouts  19.7 us (6%)
  between operations  14.9 us (5%)
  other arithmetic  9.53 us (3%)
    ppermute x16, starting transfers between devices, from_behind(): lax.ppermute(value, axis, [(source, source + steps) for source in range(f...  60.1 us
    reduce_scatter x1, waiting for transfers between devices, per_device(): lax.psum_scatter(terms.astype(jnp.bfloat16), 'mp', scatter_dimension=1, t...  47.5 us
    all_gather x3, blocking collectives, mesh_update(): whole_new = lax.all_gather(part_new, 'mp', axis=1, tiled=True)  33.1 us
    all_gather x1, blocking collectives, per_device(): lax.all_gather(mesh_in, 'mp', axis=1, tiled=True)  29.5 us
    ppermute x16, waiting for transfers between devices, from_behind(): lax.ppermute(value, axis, [(source, source + steps) for source in range(f...  26.9 us
    dot_general x12, matrix products, project(): jnp.dot(inputs, weight, preferred_element_type=jnp.float32)  16.3 us
    all_to_all x2, waiting for transfers between devices, summed_on_arrival(): lax.all_to_all(pieces, axis, split_axis=0, concat_axis=0, tiled=True)  15 us
    all_to_all x1, blocking collectives, summed_on_arrival(): lax.all_to_all(pieces, axis, split_axis=0, concat_axis=0, tiled=True)  9.33 us
  transfers between devices with their start and end apart: 20, of which 10 were waited for; matrix products, arithmetic and copies ran while one was open for 4% of the time, Pallas kernels for 0%

profile of v1, /device:TPU:1, one launch (start us, length us, event | category | flops | bytes accessed | tf_op | source)
XLA Modules:
  0.0 308.1 jit_solution(10817980402256897691)
XLA Ops:
  7.2 1.2 copy.73
  8.4 1.6 stack.2
  10.0 5.1 %all-to-all-start = ((bf16[4,1024,256]{1,2,0:T(8,128)(2,1)}), bf16[4,1024,256]{1,2,0:T(8,128)(2,1)S(1)}, u32[]{:S(2)}, u32[]{:S(2)}) async-start(bf16[4,1024,256]{1,2,0:T(8,128)(2,1)} %stack.2), calls=%async_computation | async-start | bytes 4194304 | tf_op jit(solution)/shard_map/all_to_all | solution.py:109
  15.2 29.5 %all_gather.12 = bf16[256,1024]{1,0:T(8,128)(2,1)S(1)} all-gather(bf16[256,256]{1,0:T(8,128)(2,1)S(1)} %copy-done.3), channel_id=1, replica_groups=mesh['nodes'=128,'mp'=4] {'mp'}, dimensions={1}, use_global_device_ids=true | all-gather | bytes 655360 | tf_op jit(solution)/shard_map/all_gather | solution.py:111
  45.5 1.3 convolution_convert_fusion.19
  47.8 2.2 fusion.9
  50.0 1.4 convolution_convert_fusion.6
  51.4 1.4 convolution_convert_fusion.7
  52.9 0.8 pad_maximum_fusion
  53.7 9.1 %collective-permute-start.1 = (bf16[1024,256]{0,1:T(8,128)(2,1)}, bf16[1024,256]{0,1:T(8,128)(2,1)}, u32[]{:S(2)}, u32[]{:S(2)}) collective-permute-start(bf16[1024,256]{0,1:T(8,128)(2,1)} %pad_maximum_fusion), channel_id=1, source_target_pairs={{0,4},{4,8},{8,12},{12,16},{16,20},{20,24},{24,28},{28,32},{32,36}... | collective-permute-start | bytes 1572872 | tf_op jit(solution)/shard_map/ppermute | solution.py:27
  62.8 3.9 %collective-permute-start = (bf16[1024,256]{0,1:T(8,128)(2,1)}, bf16[1024,256]{0,1:T(8,128)(2,1)}, u32[]{:S(2)}, u32[]{:S(2)}) collective-permute-start(bf16[1024,256]{0,1:T(8,128)(2,1)} %pad_maximum_fusion), channel_id=1, source_target_pairs={{0,8},{4,12},{8,16},{12,20},{16,24},{20,28},{24,32},{28,36},{32,40... | collective-permute-start | bytes 1572872 | tf_op jit(solution)/shard_map/ppermute | solution.py:27
  66.7 1.9 collective-permute-start.2
  68.8 1.3 collective-permute-start.3
  70.2 10.2 %collective-permute-done = bf16[1024,256]{0,1:T(8,128)(2,1)} collective-permute-done((bf16[1024,256]{0,1:T(8,128)(2,1)}, bf16[1024,256]{0,1:T(8,128)(2,1)}, u32[]{:S(2)}, u32[]{:S(2)}) %collective-permute-start) | collective-permute-done | bytes 524320 | tf_op jit(solution)/shard_map/ppermute | solution.py:27
  80.4 1.1 constant_dynamic-update-slice_fusion.4
  81.5 1.1 constant_dynamic-update-slice_fusion.3
  82.7 1.1 constant_dynamic-update-slice_fusion.1
  83.8 1.2 collective-permute-done.3
  85.0 1.1 constant_dynamic-update-slice_fusion
  86.0 2.6 copy.100
  88.6 2.3 gather_fusion
  92.0 1.1 fusion.28
  93.6 0.8 copy.173
  94.4 3.5 %all-to-all-start.1 = ((bf16[4,256,256]{2,1,0:T(8,128)(2,1)}), bf16[4,256,256]{2,1,0:T(8,128)(2,1)S(1)}, u32[]{:S(2)}, u32[]{:S(2)}) async-start(bf16[4,256,256]{2,1,0:T(8,128)(2,1)} %bitcast.170), calls=%async_computation.1 | async-start | bytes 1048576 | tf_op jit(solution)/shard_map/all_to_all | solution.py:20
  98.2 6.6 %all-to-all-done.1 = bf16[4,256,256]{2,1,0:T(8,128)(2,1)S(1)} async-done(((bf16[4,256,256]{2,1,0:T(8,128)(2,1)}), bf16[4,256,256]{2,1,0:T(8,128)(2,1)S(1)}, u32[]{:S(2)}, u32[]{:S(2)}) %all-to-all-start.1) | async-done | bytes 524320 | tf_op jit(solution)/shard_map/all_to_all | solution.py:20
  104.9 11.0 %all_gather.13 = bf16[256,1024]{1,0:T(8,128)(2,1)S(1)} all-gather(bf16[256,256]{1,0:T(8,128)(2,1)S(1)} %add_convert_fusion.2), channel_id=1, replica_groups=mesh['nodes'=128,'mp'=4] {'mp'}, dimensions={1}, use_global_device_ids=true | all-gather | bytes 655360 | tf_op jit(solution)/shard_map/all_gather | solution.py:121
  116.6 1.3 convolution_convert_fusion.16
  117.9 1.3 convolution_convert_fusion.17
  119.2 9.9 %collective-permute-start.5 = (bf16[256,256]{0,1:T(8,128)(2,1)S(1)}, bf16[256,256]{0,1:T(8,128)(2,1)S(1)}, u32[]{:S(2)}, u32[]{:S(2)}) collective-permute-start(bf16[256,256]{0,1:T(8,128)(2,1)S(1)} %pad_maximum_fusion.1), channel_id=1, source_target_pairs={{0,4},{4,8},{8,12},{12,16},{16,20},{20,24},{24,28},{28,32},{32,36}... | collective-permute-start | bytes 393224 | tf_op jit(solution)/shard_map/ppermute | solution.py:27
  129.1 3.6 %collective-permute-start.4 = (bf16[256,256]{0,1:T(8,128)(2,1)S(1)}, bf16[256,256]{0,1:T(8,128)(2,1)S(1)}, u32[]{:S(2)}, u32[]{:S(2)}) collective-permute-start(bf16[256,256]{0,1:T(8,128)(2,1)S(1)} %pad_maximum_fusion.1), channel_id=1, source_target_pairs={{0,8},{4,12},{8,16},{12,20},{16,24},{20,28},{24,32},{28,36},{32,40... | collective-permute-start | bytes 393224 | tf_op jit(solution)/shard_map/ppermute | solution.py:27
  132.7 1.2 convolution_convert_fusion.15
  134.0 1.3 collective-permute-start.7
  135.3 1.9 collective-permute-start.6
  137.4 5.5 %collective-permute-done.6 = bf16[256,256]{0,1:T(8,128)(2,1)S(1)} collective-permute-done((bf16[256,256]{0,1:T(8,128)(2,1)S(1)}, bf16[256,256]{0,1:T(8,128)(2,1)S(1)}, u32[]{:S(2)}, u32[]{:S(2)}) %collective-permute-start.6) | collective-permute-done | bytes 131104 | tf_op jit(solution)/shard_map/ppermute | solution.py:27
  145.1 1.0 fusion.29
  146.6 9.3 %all_to_all.20 = bf16[4,256,256]{2,1,0:T(8,128)(2,1)S(1)} all-to-all(bf16[4,256,256]{2,1,0:T(8,128)(2,1)S(1)} %bitcast.181), channel_id=1, replica_groups=mesh['nodes'=128,'mp'=4] {'mp'}, dimensions={0} | all-to-all | bytes 1048576 | tf_op jit(solution)/shard_map/all_to_all | solution.py:20
  156.0 11.0 %all_gather.14 = bf16[256,1024]{1,0:T(8,128)(2,1)S(1)} all-gather(bf16[256,256]{1,0:T(8,128)(2,1)S(1)} %add_convert_fusion.1), channel_id=1, replica_groups=mesh['nodes'=128,'mp'=4] {'mp'}, dimensions={1}, use_global_device_ids=true | all-gather | bytes 655360 | tf_op jit(solution)/shard_map/all_gather | solution.py:121
  167.8 1.3 convolution_convert_fusion.12
  169.1 1.3 convolution_convert_fusion.13
  170.4 7.4 %collective-permute-start.9 = (bf16[256,256]{0,1:T(8,128)(2,1)S(1)}, bf16[256,256]{0,1:T(8,128)(2,1)S(1)}, u32[]{:S(2)}, u32[]{:S(2)}) collective-permute-start(bf16[256,256]{0,1:T(8,128)(2,1)S(1)} %pad_maximum_fusion.2), channel_id=1, source_target_pairs={{0,4},{4,8},{8,12},{12,16},{16,20},{20,24},{24,28},{28,32},{32,36}... | collective-permute-start | bytes 393224 | tf_op jit(solution)/shard_map/ppermute | solution.py:27
  177.8 4.7 %collective-permute-start.8 = (bf16[256,256]{0,1:T(8,128)(2,1)S(1)}, bf16[256,256]{0,1:T(8,128)(2,1)S(1)}, u32[]{:S(2)}, u32[]{:S(2)}) collective-permute-start(bf16[256,256]{0,1:T(8,128)(2,1)S(1)} %pad_maximum_fusion.2), channel_id=1, source_target_pairs={{0,8},{4,12},{8,16},{12,20},{16,24},{20,28},{24,32},{28,36},{32,40... | collective-permute-start | bytes 393224 | tf_op jit(solution)/shard_map/ppermute | solution.py:27
  182.5 1.2 convolution_convert_fusion.11
  183.7 1.3 collective-permute-start.11
  185.0 1.9 collective-permute-start.10
  187.2 4.2 %collective-permute-done.10 = bf16[256,256]{0,1:T(8,128)(2,1)S(1)} collective-permute-done((bf16[256,256]{0,1:T(8,128)(2,1)S(1)}, bf16[256,256]{0,1:T(8,128)(2,1)S(1)}, u32[]{:S(2)}, u32[]{:S(2)}) %collective-permute-start.10) | collective-permute-done | bytes 131104 | tf_op jit(solution)/shard_map/ppermute | solution.py:27
  193.5 1.0 fusion.30
  194.9 0.8 copy.171
  195.8 3.5 %all-to-all-start.3 = ((bf16[4,256,256]{2,1,0:T(8,128)(2,1)}), bf16[4,256,256]{2,1,0:T(8,128)(2,1)S(1)}, u32[]{:S(2)}, u32[]{:S(2)}) async-start(bf16[4,256,256]{2,1,0:T(8,128)(2,1)} %bitcast.166), calls=%async_computation.3 | async-start | bytes 1048576 | tf_op jit(solution)/shard_map/all_to_all | solution.py:20
  199.4 8.4 %all-to-all-done.3 = bf16[4,256,256]{2,1,0:T(8,128)(2,1)S(1)} async-done(((bf16[4,256,256]{2,1,0:T(8,128)(2,1)}), bf16[4,256,256]{2,1,0:T(8,128)(2,1)S(1)}, u32[]{:S(2)}, u32[]{:S(2)}) %all-to-all-start.3) | async-done | bytes 524320 | tf_op jit(solution)/shard_map/all_to_all | solution.py:20
  207.9 11.1 %all_gather.15 = bf16[256,1024]{1,0:T(8,128)(2,1)S(1)} all-gather(bf16[256,256]{1,0:T(8,128)(2,1)S(1)} %add_convert_fusion), channel_id=1, replica_groups=mesh['nodes'=128,'mp'=4] {'mp'}, dimensions={1}, use_global_device_ids=true | all-gather | bytes 655360 | tf_op jit(solution)/shard_map/all_gather | solution.py:121
  219.5 1.5 convolution_convert_fusion.8
  221.0 1.4 convolution_convert_fusion.9
  222.4 4.8 %collective-permute-start.13 = (bf16[256,256]{0,1:T(8,128)(2,1)S(1)}, bf16[256,256]{0,1:T(8,128)(2,1)S(1)}, u32[]{:S(2)}, u32[]{:S(2)}) collective-permute-start(bf16[256,256]{0,1:T(8,128)(2,1)S(1)} %pad_maximum_fusion.3), channel_id=1, source_target_pairs={{0,4},{4,8},{8,12},{12,16},{16,20},{20,24},{24,28},{28,32},{32,36}... | collective-permute-start | bytes 393224 | tf_op jit(solution)/shard_map/ppermute | solution.py:27
  227.2 3.8 %collective-permute-start.12 = (bf16[256,256]{0,1:T(8,128)(2,1)S(1)}, bf16[256,256]{0,1:T(8,128)(2,1)S(1)}, u32[]{:S(2)}, u32[]{:S(2)}) collective-permute-start(bf16[256,256]{0,1:T(8,128)(2,1)S(1)} %pad_maximum_fusion.3), channel_id=1, source_target_pairs={{0,8},{4,12},{8,16},{12,20},{16,24},{20,28},{24,32},{28,36},{32,40... | collective-permute-start | bytes 393224 | tf_op jit(solution)/shard_map/ppermute | solution.py:27
  231.0 1.7 convolution_convert_fusion.5
  233.0 1.3 collective-permute-start.15
  234.3 1.9 collective-permute-start.14
  236.3 4.9 %collective-permute-done.14 = bf16[256,256]{0,1:T(8,128)(2,1)S(1)} collective-permute-done((bf16[256,256]{0,1:T(8,128)(2,1)S(1)}, bf16[256,256]{0,1:T(8,128)(2,1)S(1)}, u32[]{:S(2)}, u32[]{:S(2)}) %collective-permute-start.14) | collective-permute-done | bytes 131104 | tf_op jit(solution)/shard_map/ppermute | solution.py:27
  241.3 0.7 collective-permute-done.15
  243.6 1.0 fusion.141
  244.6 3.7 %fusion.27 = bf16[8,128,2,64]{1,3,2,0:T(8,128)(2,1)S(1)} fusion(bf16[8,256,2,64]{1,3,2,0:T(8,128)(2,1)S(1)} %bitcast.198, f32[8,2,128]{2,1,0:T(2,128)S(1)} %fusion.141, bf16[8,256,2,64]{1,3,2,0:T(8,128)(2,1)S(1)} %bitcast.197, bf16[8,128,2,64]{3,2,1,0:T(2,128)(2,1)S(1)} %reshape.320), kind=kOutput, calls=%fused_computation.55 | convolution fusion | flops 136448256 | bytes 1581056 | tf_op jit(solution)/shard_map/bhrk,bkhd->brhd/dot_general | solution.py:57
  248.5 3.1 %convolution_convert_fusion = bf16[1024,1024]{1,0:T(8,128)(2,1)} fusion(bf16[16,8,8,128]{3,2,1,0:T(8,128)(2,1)S(1)} %bitcast.189, bf16[4,128,1024]{2,1,0:T(8,128)(2,1)} %param.18), kind=kOutput, calls=%fused_computation.21 | convolution fusion | flops 269484032 | bytes 2621440 | tf_op jit(solution)/shard_map/dot_general | solution.py:150
  251.7 47.5 %reduce-scatter.2.cloned.1.call-done = bf16[1024,256]{1,0:T(8,128)(2,1)} async-done(((bf16[1024,1024]{1,0:T(8,128)(2,1)}), bf16[1024,256]{1,0:T(8,128)(2,1)}) %reduce-scatter.2.cloned.1.call-update) | async-done | bytes 524304 | tf_op jit(solution)/shard_map/reduce_scatter | solution.py:151
  299.2 2.0 select_convert_fusion
  (139 shorter events, 13.8 us)
Async XLA Ops:
  10.0 5.2 %copy-start.5 = (f32[6,1024]{1,0:T(8,128)S(1)}, f32[6,1024]{1,0:T(8,128)}, u32[]{:S(2)}) copy-start(f32[6,1024]{1,0:T(8,128)} %param.19) | copy-start | bytes 73732
  10.0 5.2 %copy-start.3 = (bf16[256,256]{1,0:T(8,128)(2,1)S(1)}, bf16[256,256]{1,0:T(8,128)(2,1)}, u32[]{:S(2)}) copy-start(bf16[256,256]{1,0:T(8,128)(2,1)} %param.14) | copy-start | bytes 393220
  10.0 34.7 %copy-start.6 = (s32[1024]{0:T(1024)S(1)}, s32[1024]{0:T(1024)}, u32[]{:S(2)}) copy-start(s32[1024]{0:T(1024)} %param.23) | copy-start | bytes 12292
  10.0 34.7 %copy-start.7 = (s32[2,4]{1,0:T(2,128)S(1)}, s32[2,4]{1,0:T(2,128)}, u32[]{:S(2)}) copy-start(s32[2,4]{1,0:T(2,128)} %param.20) | copy-start | bytes 100
  10.0 36.8 %all-to-all-start = ((bf16[4,1024,256]{1,2,0:T(8,128)(2,1)}), bf16[4,1024,256]{1,2,0:T(8,128)(2,1)S(1)}, u32[]{:S(2)}, u32[]{:S(2)}) async-start(bf16[4,1024,256]{1,2,0:T(8,128)(2,1)} %stack.2), calls=%async_computation | async-start | bytes 4194304 | tf_op jit(solution)/shard_map/all_to_all | solution.py:109
  53.7 27.8 %collective-permute-start.1 = (bf16[1024,256]{0,1:T(8,128)(2,1)}, bf16[1024,256]{0,1:T(8,128)(2,1)}, u32[]{:S(2)}, u32[]{:S(2)}) collective-permute-start(bf16[1024,256]{0,1:T(8,128)(2,1)} %pad_maximum_fusion), channel_id=1, source_target_pairs={{0,4},{4,8},{8,12},{12,16},{16,20},{20,24},{24,28},{28,32},{32,36}... | collective-permute-start | bytes 1572872 | tf_op jit(solution)/shard_map/ppermute | solution.py:27
  62.8 17.7 %collective-permute-start = (bf16[1024,256]{0,1:T(8,128)(2,1)}, bf16[1024,256]{0,1:T(8,128)(2,1)}, u32[]{:S(2)}, u32[]{:S(2)}) collective-permute-start(bf16[1024,256]{0,1:T(8,128)(2,1)} %pad_maximum_fusion), channel_id=1, source_target_pairs={{0,8},{4,12},{8,16},{12,20},{16,24},{20,28},{24,32},{28,36},{32,40... | collective-permute-start | bytes 1572872 | tf_op jit(solution)/shard_map/ppermute | solution.py:27
  66.7 15.9 %collective-permute-start.2 = (bf16[1024,256]{0,1:T(8,128)(2,1)}, bf16[1024,256]{0,1:T(8,128)(2,1)}, u32[]{:S(2)}, u32[]{:S(2)}) collective-permute-start(bf16[1024,256]{0,1:T(8,128)(2,1)} %pad_maximum_fusion), channel_id=1, source_target_pairs={{4,0},{8,4},{12,8},{16,12},{20,16},{24,20},{28,24},{32,28},{36,32}... | collective-permute-start | bytes 1572872 | tf_op jit(solution)/shard_map/ppermute | solution.py:27
  68.8 16.1 %collective-permute-start.3 = (bf16[1024,256]{0,1:T(8,128)(2,1)}, bf16[1024,256]{0,1:T(8,128)(2,1)}, u32[]{:S(2)}, u32[]{:S(2)}) collective-permute-start(bf16[1024,256]{0,1:T(8,128)(2,1)} %pad_maximum_fusion), channel_id=1, source_target_pairs={{8,0},{12,4},{16,8},{20,12},{24,16},{28,20},{32,24},{36,28},{40,32... | collective-permute-start | bytes 1572872 | tf_op jit(solution)/shard_map/ppermute | solution.py:27
  92.0 1.2 copy-start.2
  93.1 4.8 %copy-start.8 = (s32[2,3]{1,0:T(2,128)S(1)}, s32[2,3]{1,0:T(2,128)}, u32[]{:S(2)}) copy-start(s32[2,3]{1,0:T(2,128)} %param.21) | copy-start | bytes 76
  93.1 4.9 %copy-start.9 = (s32[8,2]{0,1:T(2,128)S(1)}, s32[8,2]{0,1:T(2,128)}, u32[]{:S(2)}) copy-start(s32[8,2]{0,1:T(2,128)} %param.22) | copy-start | bytes 196
  94.4 10.4 %all-to-all-start.1 = ((bf16[4,256,256]{2,1,0:T(8,128)(2,1)}), bf16[4,256,256]{2,1,0:T(8,128)(2,1)S(1)}, u32[]{:S(2)}, u32[]{:S(2)}) async-start(bf16[4,256,256]{2,1,0:T(8,128)(2,1)} %bitcast.170), calls=%async_computation.1 | async-start | bytes 1048576 | tf_op jit(solution)/shard_map/all_to_all | solution.py:20
  119.2 18.2 %collective-permute-start.5 = (bf16[256,256]{0,1:T(8,128)(2,1)S(1)}, bf16[256,256]{0,1:T(8,128)(2,1)S(1)}, u32[]{:S(2)}, u32[]{:S(2)}) collective-permute-start(bf16[256,256]{0,1:T(8,128)(2,1)S(1)} %pad_maximum_fusion.1), channel_id=1, source_target_pairs={{0,4},{4,8},{8,12},{12,16},{16,20},{20,24},{24,28},{28,32},{32,36}... | collective-permute-start | bytes 393224 | tf_op jit(solution)/shard_map/ppermute | solution.py:27
  129.1 8.2 %collective-permute-start.4 = (bf16[256,256]{0,1:T(8,128)(2,1)S(1)}, bf16[256,256]{0,1:T(8,128)(2,1)S(1)}, u32[]{:S(2)}, u32[]{:S(2)}) collective-permute-start(bf16[256,256]{0,1:T(8,128)(2,1)S(1)} %pad_maximum_fusion.1), channel_id=1, source_target_pairs={{0,8},{4,12},{8,16},{12,20},{16,24},{20,28},{24,32},{28,36},{32,40... | collective-permute-start | bytes 393224 | tf_op jit(solution)/shard_map/ppermute | solution.py:27
  134.0 9.0 %collective-permute-start.7 = (bf16[256,256]{0,1:T(8,128)(2,1)S(1)}, bf16[256,256]{0,1:T(8,128)(2,1)S(1)}, u32[]{:S(2)}, u32[]{:S(2)}) collective-permute-start(bf16[256,256]{0,1:T(8,128)(2,1)S(1)} %pad_maximum_fusion.1), channel_id=1, source_target_pairs={{8,0},{12,4},{16,8},{20,12},{24,16},{28,20},{32,24},{36,28},{40,32... | collective-permute-start | bytes 393224 | tf_op jit(solution)/shard_map/ppermute | solution.py:27
  135.3 7.6 %collective-permute-start.6 = (bf16[256,256]{0,1:T(8,128)(2,1)S(1)}, bf16[256,256]{0,1:T(8,128)(2,1)S(1)}, u32[]{:S(2)}, u32[]{:S(2)}) collective-permute-start(bf16[256,256]{0,1:T(8,128)(2,1)S(1)} %pad_maximum_fusion.1), channel_id=1, source_target_pairs={{4,0},{8,4},{12,8},{16,12},{20,16},{24,20},{28,24},{32,28},{36,32}... | collective-permute-start | bytes 393224 | tf_op jit(solution)/shard_map/ppermute | solution.py:27
  170.4 16.8 %collective-permute-start.9 = (bf16[256,256]{0,1:T(8,128)(2,1)S(1)}, bf16[256,256]{0,1:T(8,128)(2,1)S(1)}, u32[]{:S(2)}, u32[]{:S(2)}) collective-permute-start(bf16[256,256]{0,1:T(8,128)(2,1)S(1)} %pad_maximum_fusion.2), channel_id=1, source_target_pairs={{0,4},{4,8},{8,12},{12,16},{16,20},{20,24},{24,28},{28,32},{32,36}... | collective-permute-start | bytes 393224 | tf_op jit(solution)/shard_map/ppermute | solution.py:27
  177.8 9.3 %collective-permute-start.8 = (bf16[256,256]{0,1:T(8,128)(2,1)S(1)}, bf16[256,256]{0,1:T(8,128)(2,1)S(1)}, u32[]{:S(2)}, u32[]{:S(2)}) collective-permute-start(bf16[256,256]{0,1:T(8,128)(2,1)S(1)} %pad_maximum_fusion.2), channel_id=1, source_target_pairs={{0,8},{4,12},{8,16},{12,20},{16,24},{20,28},{24,32},{28,36},{32,40... | collective-permute-start | bytes 393224 | tf_op jit(solution)/shard_map/ppermute | solution.py:27
  183.7 7.7 %collective-permute-start.11 = (bf16[256,256]{0,1:T(8,128)(2,1)S(1)}, bf16[256,256]{0,1:T(8,128)(2,1)S(1)}, u32[]{:S(2)}, u32[]{:S(2)}) collective-permute-start(bf16[256,256]{0,1:T(8,128)(2,1)S(1)} %pad_maximum_fusion.2), channel_id=1, source_target_pairs={{8,0},{12,4},{16,8},{20,12},{24,16},{28,20},{32,24},{36,28},{40,32... | collective-permute-start | bytes 393224 | tf_op jit(solution)/shard_map/ppermute | solution.py:27
  185.0 6.4 %collective-permute-start.10 = (bf16[256,256]{0,1:T(8,128)(2,1)S(1)}, bf16[256,256]{0,1:T(8,128)(2,1)S(1)}, u32[]{:S(2)}, u32[]{:S(2)}) collective-permute-start(bf16[256,256]{0,1:T(8,128)(2,1)S(1)} %pad_maximum_fusion.2), channel_id=1, source_target_pairs={{4,0},{8,4},{12,8},{16,12},{20,16},{24,20},{28,24},{32,28},{36,32}... | collective-permute-start | bytes 393224 | tf_op jit(solution)/shard_map/ppermute | solution.py:27
  195.8 12.0 %all-to-all-start.3 = ((bf16[4,256,256]{2,1,0:T(8,128)(2,1)}), bf16[4,256,256]{2,1,0:T(8,128)(2,1)S(1)}, u32[]{:S(2)}, u32[]{:S(2)}) async-start(bf16[4,256,256]{2,1,0:T(8,128)(2,1)} %bitcast.166), calls=%async_computation.3 | async-start | bytes 1048576 | tf_op jit(solution)/shard_map/all_to_all | solution.py:20
  199.3 100.0 %reduce-scatter.2.cloned.1.call-start = ((), (), s32[]{:S(2)}) async-start(), calls=%async_computation.5 | async-start | bytes 2621440 | tf_op jit(solution)/shard_map/reduce_scatter | solution.py:151
  207.9 14.5 %copy-start.4 = (bf16[256,256]{1,0:T(8,128)(2,1)}, bf16[256,256]{1,0:T(8,128)(2,1)S(1)}, u32[]{:S(2)}) copy-start(bf16[256,256]{1,0:T(8,128)(2,1)S(1)} %add_convert_fusion) | copy-start | bytes 393220
  219.0 12.0 %copy-start = (bf16[4,1024,256]{1,2,0:T(8,128)(2,1)S(1)}, bf16[4,1024,256]{1,2,0:T(8,128)(2,1)}, u32[]{:S(2)}) copy-start(bf16[4,1024,256]{1,2,0:T(8,128)(2,1)} %get-tuple-element.11) | copy-start | bytes 6291460
  222.4 13.9 %collective-permute-start.13 = (bf16[256,256]{0,1:T(8,128)(2,1)S(1)}, bf16[256,256]{0,1:T(8,128)(2,1)S(1)}, u32[]{:S(2)}, u32[]{:S(2)}) collective-permute-start(bf16[256,256]{0,1:T(8,128)(2,1)S(1)} %pad_maximum_fusion.3), channel_id=1, source_target_pairs={{0,4},{4,8},{8,12},{12,16},{16,20},{20,24},{24,28},{28,32},{32,36}... | collective-permute-start | bytes 393224 | tf_op jit(solution)/shard_map/ppermute | solution.py:27
  227.2 9.0 %collective-permute-start.12 = (bf16[256,256]{0,1:T(8,128)(2,1)S(1)}, bf16[256,256]{0,1:T(8,128)(2,1)S(1)}, u32[]{:S(2)}, u32[]{:S(2)}) collective-permute-start(bf16[256,256]{0,1:T(8,128)(2,1)S(1)} %pad_maximum_fusion.3), channel_id=1, source_target_pairs={{0,8},{4,12},{8,16},{12,20},{16,24},{20,28},{24,32},{28,36},{32,40... | collective-permute-start | bytes 393224 | tf_op jit(solution)/shard_map/ppermute | solution.py:27
  233.0 9.0 %collective-permute-start.15 = (bf16[256,256]{0,1:T(8,128)(2,1)S(1)}, bf16[256,256]{0,1:T(8,128)(2,1)S(1)}, u32[]{:S(2)}, u32[]{:S(2)}) collective-permute-start(bf16[256,256]{0,1:T(8,128)(2,1)S(1)} %pad_maximum_fusion.3), channel_id=1, source_target_pairs={{8,0},{12,4},{16,8},{20,12},{24,16},{28,20},{32,24},{36,28},{40,32... | collective-permute-start | bytes 393224 | tf_op jit(solution)/shard_map/ppermute | solution.py:27
  234.3 6.9 %collective-permute-start.14 = (bf16[256,256]{0,1:T(8,128)(2,1)S(1)}, bf16[256,256]{0,1:T(8,128)(2,1)S(1)}, u32[]{:S(2)}, u32[]{:S(2)}) collective-permute-start(bf16[256,256]{0,1:T(8,128)(2,1)S(1)} %pad_maximum_fusion.3), channel_id=1, source_target_pairs={{4,0},{8,4},{12,8},{16,12},{20,16},{24,20},{28,24},{32,28},{36,32}... | collective-permute-start | bytes 393224 | tf_op jit(solution)/shard_map/ppermute | solution.py:27
  248.5 50.8 %copy-start.1 = (bf16[1024,256]{1,0:T(8,128)(2,1)S(1)}, bf16[1024,256]{1,0:T(8,128)(2,1)}, u32[]{:S(2)}) copy-start(bf16[1024,256]{1,0:T(8,128)(2,1)} %param.13) | copy-start | bytes 1572868
Sparse Core Ops, SparseCore 0:
  251.7 47.4 reduce-scatter.1
